TPU v7x, 32 devices: a whole 2x2x4 slice. The times are simulated.
32 devices in a mesh: rep: 8 (over y, x, core), fsdp: 4 (over z).
Axes of the slice: x: 2, y: 2, z: 4, core: 2. Of those that a mesh axis runs over, the one named last changes fastest.
Arguments:
- tokens: bfloat16 [16384, 768], P(('rep', 'fsdp')), may hold values from -6 to 6
- cotangent: bfloat16 [16384, 768], P(('rep', 'fsdp')), may hold values from -6 to 6
- lengths: int32 [32], P(('rep', 'fsdp')), may hold values from 1 to 512, 10240 in all
- slot_seq: int32 [32], replicated, may hold values from 0 to 31, each once
- query_weight: bfloat16 [768, 768], P('fsdp'), may hold values from -0.21875 to 0.21875
- query_bias: bfloat16 [768], P('fsdp'), may hold values from -2 to 2
- key_weight: bfloat16 [768, 768], P('fsdp'), may hold values from -0.21875 to 0.21875
- value_weight: bfloat16 [768, 768], P('fsdp'), may hold values from -0.21875 to 0.21875
- value_bias: bfloat16 [768], P('fsdp'), may hold values from -2 to 2
- out_weight: bfloat16 [768, 768], P('fsdp'), may hold values from -2.5 to 2.5
- out_bias: bfloat16 [768], P('fsdp'), may hold values from -2 to 2
- first_gain: bfloat16 [768], P('fsdp'), may hold values from 0.5 to 1.5
- first_shift: bfloat16 [768], P('fsdp'), may hold values from -2 to 2
- inner_weight: bfloat16 [768, 3072], P('fsdp'), may hold values from -0.21875 to 0.21875
- inner_bias: bfloat16 [3072], P('fsdp'), may hold values from -2 to 2
- outer_weight: bfloat16 [3072, 768], P('fsdp'), may hold values from -0.109375 to 0.109375
- outer_bias: bfloat16 [768], P('fsdp'), may hold values from -2 to 2
- second_gain: bfloat16 [768], P('fsdp'), may hold values from 0.5 to 1.5
- second_shift: bfloat16 [768], P('fsdp'), may hold values from -2 to 2
Outputs:
- output: bfloat16 [16384, 768], P(('rep', 'fsdp'))
- grad_tokens: bfloat16 [16384, 768], P(('rep', 'fsdp'))
- query_weight_grad: float32 [768, 768], P('fsdp')
- query_bias_grad: float32 [768], P('fsdp')
- key_weight_grad: float32 [768, 768], P('fsdp')
- value_weight_grad: float32 [768, 768], P('fsdp')
- value_bias_grad: float32 [768], P('fsdp')
- out_weight_grad: float32 [768, 768], P('fsdp')
- out_bias_grad: float32 [768], P('fsdp')
- first_gain_grad: float32 [768], P('fsdp')
- first_shift_grad: float32 [768], P('fsdp')
- inner_weight_grad: float32 [768, 3072], P('fsdp')
- inner_bias_grad: float32 [3072], P('fsdp')
- outer_weight_grad: float32 [3072, 768], P('fsdp')
- outer_bias_grad: float32 [768], P('fsdp')
- second_gain_grad: float32 [768], P('fsdp')
- second_shift_grad: float32 [768], P('fsdp')
Inputs may be any that keep to these rules, and one draw needn't show every extreme that they name: Every sequence has at least one token; the longest has exactly 512; the lengths add up to 10240. `slot_seq`: each sequence fills exactly one slot.
All inputs are finite; a program needn't handle non-finite values. No bound on the sum of `lengths` on one device may be relied on, other than what follows from the above.
Results may differ from a plain program's by a relative error of at most 0.017.
Values may be sent and summed in bfloat16 or wider, within the bound.
A program may use at most 128 MiB of HBM per device.

v0:
```python
import math
import jax
import jax.numpy as jnp
from jax import lax
from jax.sharding import PartitionSpec as P

HEADS = 12
HD = 64
norm_eps = 1e-12
masked_score = -1e30
inv_root_two = 0.7071067811865476
inv_root_two_pi = 0.3989422804014327


def matmul(left, right):
    return jnp.dot(left, right, preferred_element_type=jnp.float32)


def matmul_left_t(left, right):
    return lax.dot_general(
        left, right, (((0,), (0,)), ((), ())), preferred_element_type=jnp.float32
    )


def matmul_right_t(left, right):
    return lax.dot_general(
        left, right, (((1,), (1,)), ((), ())), preferred_element_type=jnp.float32
    )


def norm_forward(values, norm_gain, norm_shift):
    center = values - jnp.mean(values, axis=-1, keepdims=True)
    spread = jnp.mean(center * center, axis=-1, keepdims=True)
    scaled_inv = lax.rsqrt(spread + norm_eps)
    normed = center * scaled_inv
    return (normed * norm_gain + norm_shift, normed, scaled_inv)


def norm_backward(grad_out, normed, scaled_inv, norm_gain):
    grad_normed = grad_out * norm_gain
    first_mean = jnp.mean(grad_normed, axis=-1, keepdims=True)
    second_mean = jnp.mean(grad_normed * normed, axis=-1, keepdims=True)
    return (grad_normed - first_mean - normed * second_mean) * scaled_inv


def score_block(query_block, key_rows, kept_keys):
    scores = jnp.einsum(
        "qhd,khd->hqk", query_block, key_rows, preferred_element_type=jnp.float32
    ) * HD ** (-0.5)
    return jnp.where(kept_keys[None, None, :], scores, masked_score)


def attention_forward(query_rows, key_rows, value_rows, kept_keys, block_rows):
    seq_len = query_rows.shape[0]

    def one_block(query_block):
        scores = score_block(query_block, key_rows, kept_keys)
        largest = jnp.max(scores, axis=-1, keepdims=True)
        weights = jnp.exp(scores - largest)
        row_total = jnp.sum(weights, axis=-1, keepdims=True)
        chances = (weights / row_total).astype(jnp.bfloat16)
        context = jnp.einsum(
            "hqk,khd->qhd", chances, value_rows, preferred_element_type=jnp.float32
        )
        return (context, largest + jnp.log(row_total))

    blocks = query_rows.reshape(seq_len // block_rows, block_rows, HEADS, HD)
    context, log_total = lax.map(one_block, blocks)
    return (context.reshape(seq_len, HEADS * HD), log_total)


def attention_backward(
    query_rows, key_rows, value_rows, kept_keys, grad_context, log_total, block_rows
):
    seq_len = query_rows.shape[0]
    block_count = seq_len // block_rows
    scale = HD ** (-0.5)

    def one_block(carry, item):
        grad_keys, grad_values = carry
        query_block, grad_block, log_block = item
        scores = score_block(query_block, key_rows, kept_keys)
        chances = jnp.exp(scores - log_block)
        grad_chances = jnp.einsum(
            "qhd,khd->hqk", grad_block, value_rows, preferred_element_type=jnp.float32
        )
        centered = jnp.sum(chances * grad_chances, axis=-1, keepdims=True)
        grad_scores = (chances * (grad_chances - centered)).astype(jnp.bfloat16)
        grad_query = (
            jnp.einsum("hqk,khd->qhd", grad_scores, key_rows, preferred_element_type=jnp.float32)
            * scale
        )
        grad_keys = (
            grad_keys
            + jnp.einsum(
                "hqk,qhd->khd", grad_scores, query_block, preferred_element_type=jnp.float32
            )
            * scale
        )
        grad_values = grad_values + jnp.einsum(
            "hqk,qhd->khd",
            chances.astype(jnp.bfloat16),
            grad_block,
            preferred_element_type=jnp.float32,
        )
        return ((grad_keys, grad_values), grad_query)

    start = jnp.zeros(key_rows.shape, jnp.float32)
    items = (
        query_rows.reshape(block_count, block_rows, HEADS, HD),
        grad_context.reshape(block_count, block_rows, HEADS, HD),
        log_total,
    )
    (grad_keys, grad_values), grad_query = lax.scan(one_block, (start, start), items)
    return (
        grad_query.reshape(seq_len, HEADS * HD),
        grad_keys.reshape(seq_len, HEADS * HD),
        grad_values.reshape(seq_len, HEADS * HD),
    )


def shards(
    tokens,
    cotangent,
    lengths,
    slot_seq,
    query_weight,
    query_bias,
    key_weight,
    value_weight,
    value_bias,
    out_weight,
    out_bias,
    first_gain,
    first_shift,
    inner_weight,
    inner_bias,
    outer_weight,
    outer_bias,
    second_gain,
    second_shift,
):
    peer_count = lax.axis_size(("rep", "fsdp"))
    row_count, feature_dim = tokens.shape
    piece_rows = row_count // peer_count
    slots = jnp.arange(peer_count, dtype=jnp.int32)
    inverse = jnp.sum(jnp.where(slot_seq[None, :] == slots[:, None], slots[None, :], 0), axis=1)

    def outgoing(array):
        return jnp.take(
            array.reshape(peer_count, piece_rows, feature_dim), inverse, axis=0
        ).reshape(row_count, feature_dim)

    def incoming(array):
        return jnp.take(
            array.reshape(peer_count, piece_rows, feature_dim), slot_seq, axis=0
        ).reshape(row_count, feature_dim)

    seq_rows, seq_seed = (
        lax.all_to_all(outgoing(tokens), ("rep", "fsdp"), split_axis=0, concat_axis=0, tiled=True),
        lax.all_to_all(
            outgoing(cotangent), ("rep", "fsdp"), split_axis=0, concat_axis=0, tiled=True
        ),
    )
    kept = jnp.arange(row_count, dtype=jnp.int32) < lengths[0]
    (
        query_full,
        query_bias_full,
        key_full,
        value_full,
        value_bias_full,
        out_full,
        out_bias_full,
        first_gain_full,
        first_shift_full,
        inner_full,
        inner_bias_full,
        outer_full,
        outer_bias_full,
        second_gain_full,
        second_shift_full,
    ) = (
        lax.all_gather(query_weight, "fsdp", axis=0, tiled=True),
        lax.all_gather(query_bias, "fsdp", axis=0, tiled=True),
        lax.all_gather(key_weight, "fsdp", axis=0, tiled=True),
        lax.all_gather(value_weight, "fsdp", axis=0, tiled=True),
        lax.all_gather(value_bias, "fsdp", axis=0, tiled=True),
        lax.all_gather(out_weight, "fsdp", axis=0, tiled=True),
        lax.all_gather(out_bias, "fsdp", axis=0, tiled=True),
        lax.all_gather(first_gain, "fsdp", axis=0, tiled=True),
        lax.all_gather(first_shift, "fsdp", axis=0, tiled=True),
        lax.all_gather(inner_weight, "fsdp", axis=0, tiled=True),
        lax.all_gather(inner_bias, "fsdp", axis=0, tiled=True),
        lax.all_gather(outer_weight, "fsdp", axis=0, tiled=True),
        lax.all_gather(outer_bias, "fsdp", axis=0, tiled=True),
        lax.all_gather(second_gain, "fsdp", axis=0, tiled=True),
        lax.all_gather(second_shift, "fsdp", axis=0, tiled=True),
    )
    block_rows = math.gcd(row_count, 512)
    head_shape = (row_count, HEADS, HD)
    query_rows = (
        (matmul(seq_rows, query_full) + query_bias_full.astype(jnp.float32))
        .astype(jnp.bfloat16)
        .reshape(head_shape)
    )
    key_rows = matmul(seq_rows, key_full).astype(jnp.bfloat16).reshape(head_shape)
    value_rows = (
        (matmul(seq_rows, value_full) + value_bias_full.astype(jnp.float32))
        .astype(jnp.bfloat16)
        .reshape(head_shape)
    )
    context, log_total = attention_forward(query_rows, key_rows, value_rows, kept, block_rows)
    context = context.astype(jnp.bfloat16)
    attended = matmul(context, out_full) + out_bias_full.astype(jnp.float32)
    hidden, first_normed, first_inv = norm_forward(
        seq_rows.astype(jnp.float32) + attended,
        first_gain_full.astype(jnp.float32),
        first_shift_full.astype(jnp.float32),
    )
    hidden_low = hidden.astype(jnp.bfloat16)
    inner = matmul(hidden_low, inner_full) + inner_bias_full.astype(jnp.float32)
    activated = jax.nn.gelu(inner, approximate=False).astype(jnp.bfloat16)
    outer = matmul(activated, outer_full) + outer_bias_full.astype(jnp.float32)
    result, second_normed, second_inv = norm_forward(
        hidden + outer, second_gain_full.astype(jnp.float32), second_shift_full.astype(jnp.float32)
    )
    result = jnp.where(kept[:, None], result, 0.0).astype(jnp.bfloat16)
    (
        query_back,
        key_back,
        value_back,
        out_back,
        first_gain_back,
        inner_back,
        outer_back,
        second_gain_back,
    ) = (
        lax.all_gather(query_weight, "fsdp", axis=0, tiled=True),
        lax.all_gather(key_weight, "fsdp", axis=0, tiled=True),
        lax.all_gather(value_weight, "fsdp", axis=0, tiled=True),
        lax.all_gather(out_weight, "fsdp", axis=0, tiled=True),
        lax.all_gather(first_gain, "fsdp", axis=0, tiled=True),
        lax.all_gather(inner_weight, "fsdp", axis=0, tiled=True),
        lax.all_gather(outer_weight, "fsdp", axis=0, tiled=True),
        lax.all_gather(second_gain, "fsdp", axis=0, tiled=True),
    )
    seed_rows = jnp.where(kept[:, None], seq_seed.astype(jnp.float32), 0.0)
    grad_second_gain = jnp.sum(seed_rows * second_normed, axis=0)
    grad_second_shift = jnp.sum(seed_rows, axis=0)
    grad_second = norm_backward(
        seed_rows, second_normed, second_inv, second_gain_back.astype(jnp.float32)
    )
    grad_outer = grad_second.astype(jnp.bfloat16)
    grad_outer_bias = jnp.sum(grad_outer, axis=0, dtype=jnp.float32)
    grad_outer_weight = matmul_left_t(activated, grad_outer)
    grad_activated = matmul_right_t(grad_outer, outer_back)
    slope = (
        0.5 * (1.0 + lax.erf(inner * inv_root_two))
        + inner * jnp.exp(-0.5 * inner * inner) * inv_root_two_pi
    )
    grad_inner = (grad_activated * slope).astype(jnp.bfloat16)
    grad_inner_bias = jnp.sum(grad_inner, axis=0, dtype=jnp.float32)
    grad_inner_weight = matmul_left_t(hidden_low, grad_inner)
    grad_hidden = grad_second + matmul_right_t(grad_inner, inner_back)
    grad_first_gain = jnp.sum(grad_hidden * first_normed, axis=0)
    grad_first_shift = jnp.sum(grad_hidden, axis=0)
    grad_residual = norm_backward(
        grad_hidden, first_normed, first_inv, first_gain_back.astype(jnp.float32)
    )
    grad_attended = grad_residual.astype(jnp.bfloat16)
    grad_out_bias = jnp.sum(grad_attended, axis=0, dtype=jnp.float32)
    grad_out_weight = matmul_left_t(context, grad_attended)
    grad_context = matmul_right_t(grad_attended, out_back).astype(jnp.bfloat16)
    grad_query, grad_key, grad_value = attention_backward(
        query_rows,
        key_rows,
        value_rows,
        kept,
        grad_context.reshape(head_shape),
        log_total,
        block_rows,
    )
    grad_query = grad_query.astype(jnp.bfloat16)
    grad_key = grad_key.astype(jnp.bfloat16)
    grad_value = grad_value.astype(jnp.bfloat16)
    grad_query_bias = jnp.sum(grad_query, axis=0, dtype=jnp.float32)
    grad_value_bias = jnp.sum(grad_value, axis=0, dtype=jnp.float32)
    grad_query_weight = matmul_left_t(seq_rows, grad_query)
    grad_key_weight = matmul_left_t(seq_rows, grad_key)
    grad_value_weight = matmul_left_t(seq_rows, grad_value)
    grad_input = (
        grad_residual
        + matmul_right_t(grad_query, query_back)
        + matmul_right_t(grad_key, key_back)
        + matmul_right_t(grad_value, value_back)
    ).astype(jnp.bfloat16)
    shares = (
        lax.psum_scatter(
            grad_query_weight.astype(jnp.bfloat16), "fsdp", scatter_dimension=0, tiled=True
        ).astype(jnp.float32),
        lax.psum_scatter(
            grad_query_bias.astype(jnp.bfloat16), "fsdp", scatter_dimension=0, tiled=True
        ).astype(jnp.float32),
        lax.psum_scatter(
            grad_key_weight.astype(jnp.bfloat16), "fsdp", scatter_dimension=0, tiled=True
        ).astype(jnp.float32),
        lax.psum_scatter(
            grad_value_weight.astype(jnp.bfloat16), "fsdp", scatter_dimension=0, tiled=True
        ).astype(jnp.float32),
        lax.psum_scatter(
            grad_value_bias.astype(jnp.bfloat16), "fsdp", scatter_dimension=0, tiled=True
        ).astype(jnp.float32),
        lax.psum_scatter(
            grad_out_weight.astype(jnp.bfloat16), "fsdp", scatter_dimension=0, tiled=True
        ).astype(jnp.float32),
        lax.psum_scatter(
            grad_out_bias.astype(jnp.bfloat16), "fsdp", scatter_dimension=0, tiled=True
        ).astype(jnp.float32),
        lax.psum_scatter(
            grad_first_gain.astype(jnp.bfloat16), "fsdp", scatter_dimension=0, tiled=True
        ).astype(jnp.float32),
        lax.psum_scatter(
            grad_first_shift.astype(jnp.bfloat16), "fsdp", scatter_dimension=0, tiled=True
        ).astype(jnp.float32),
        lax.psum_scatter(
            grad_inner_weight.astype(jnp.bfloat16), "fsdp", scatter_dimension=0, tiled=True
        ).astype(jnp.float32),
        lax.psum_scatter(
            grad_inner_bias.astype(jnp.bfloat16), "fsdp", scatter_dimension=0, tiled=True
        ).astype(jnp.float32),
        lax.psum_scatter(
            grad_outer_weight.astype(jnp.bfloat16), "fsdp", scatter_dimension=0, tiled=True
        ).astype(jnp.float32),
        lax.psum_scatter(
            grad_outer_bias.astype(jnp.bfloat16), "fsdp", scatter_dimension=0, tiled=True
        ).astype(jnp.float32),
        lax.psum_scatter(
            grad_second_gain.astype(jnp.bfloat16), "fsdp", scatter_dimension=0, tiled=True
        ).astype(jnp.float32),
        lax.psum_scatter(
            grad_second_shift.astype(jnp.bfloat16), "fsdp", scatter_dimension=0, tiled=True
        ).astype(jnp.float32),
    )
    totals = lax.psum(tuple(shares), "rep")
    back_rows, back_grads = (
        lax.all_to_all(result, ("rep", "fsdp"), split_axis=0, concat_axis=0, tiled=True),
        lax.all_to_all(grad_input, ("rep", "fsdp"), split_axis=0, concat_axis=0, tiled=True),
    )
    return (incoming(back_rows), incoming(back_grads)) + tuple(totals)


def solution(mesh):
    placed = (
        P(("rep", "fsdp"), None),
        P(("rep", "fsdp"), None),
        P(("rep", "fsdp")),
        P(),
        P("fsdp", None),
        P("fsdp"),
        P("fsdp", None),
        P("fsdp", None),
        P("fsdp"),
        P("fsdp", None),
        P("fsdp"),
        P("fsdp"),
        P("fsdp"),
        P("fsdp", None),
        P("fsdp"),
        P("fsdp", None),
        P("fsdp"),
        P("fsdp"),
        P("fsdp"),
    )
    return jax.shard_map(
        shards,
        mesh=mesh,
        in_specs=placed,
        out_specs=(
            P(("rep", "fsdp"), None),
            P(("rep", "fsdp"), None),
            P("fsdp", None),
            P("fsdp"),
            P("fsdp", None),
            P("fsdp", None),
            P("fsdp"),
            P("fsdp", None),
            P("fsdp"),
            P("fsdp"),
            P("fsdp"),
            P("fsdp", None),
            P("fsdp"),
            P("fsdp", None),
            P("fsdp"),
            P("fsdp"),
            P("fsdp"),
        ),
        check_vma=False,
    )
```

profile of v0, /device:TPU:0, one launch (start us, length us, event | category | flops | bytes accessed | tf_op | source)
XLA Modules:
  0.0 826.6 jit_solution(8898270440098371738)
XLA Ops:
  13.2 44.4 %all_to_all.33 = bf16[32,16,768]{2,1,0:T(8,128)(2,1)S(1)} all-to-all(bf16[32,16,768]{2,1,0:T(8,128)(2,1)S(1)} %get-tuple-element.117), channel_id=1, replica_groups=mesh['rep'=8,'fsdp'=4] {'rep','fsdp'}, dimensions={0} | all-to-all | bytes 1572864 | tf_op jit(solution)/shard_map/all_to_all | solution.py:161
  65.5 40.4 %all-reduce.19 = (bf16[768]{0:T(1024)(128)(2,1)S(1)}, bf16[768]{0:T(1024)(128)(2,1)S(1)}, bf16[768]{0:T(1024)(128)(2,1)S(1)}, bf16[768]{0:T(1024)(128)(2,1)S(1)}...) all-reduce(bf16[768]{0:T(1024)(128)(2,1)S(1)} %dynamic-update-slice, ...), channel_id=1, replica_groups=mesh['rep'=8,'fsdp'=4] {'fsdp'}, use_global_device_ids=true, to_apply=%add | all-reduce | flops 5376 | bytes 21504
  106.0 14.0 %all-gather = bf16[4,1,768]{2,1,0:T(2,128)(2,1)S(1)} all-gather(bf16[1,1,768]{2,1,0:T(2,128)(2,1)S(1)} %reshape.251), channel_id=1, replica_groups=mesh['rep'=8,'fsdp'=4] {'fsdp'}, dimensions={0}, use_global_device_ids=true | all-gather | bytes 7680 | tf_op jit(solution)/shard_map/all_gather | solution.py:193
  130.9 4.5 copy-done.2
  141.6 8.0 fusion.27
  149.6 13.9 %all-gather.14.cloned.1.call-done = bf16[768,768]{1,0:T(8,128)(2,1)} async-done(((bf16[192,768]{1,0:T(8,128)(2,1)}), bf16[768,768]{1,0:T(8,128)(2,1)}) %all-gather.14.cloned.1.call-update) | async-done | bytes 1179664 | tf_op jit(solution)/shard_map/all_gather | solution.py:188
  166.5 87.1 %all-gather.16.cloned.1.call-done = bf16[768,3072]{1,0:T(8,128)(2,1)} async-done(((bf16[192,3072]{1,0:T(8,128)(2,1)}), bf16[768,3072]{1,0:T(8,128)(2,1)}) %all-gather.16.cloned.1.call-update) | async-done | bytes 4718608 | tf_op jit(solution)/shard_map/all_gather | solution.py:192
  253.6 19.3 %fusion.4 = (bf16[512,3072]{1,0:T(8,128)(2,1)}, f32[512,3072]{1,0:T(8,128)}) fusion(f32[3072]{0:T(1024)S(1)} %bitcast.109, bf16[768,3072]{1,0:T(8,128)(2,1)} %all-gather.16.cloned.1.call-done, f32[512,768]{1,0:T(8,128)S(1)} %get-tuple-element.122, f32[768]{0:T(1024)S(1)} %convert_element_type.228, f32[768]{0:T(1024)S(1)} %convert_element_type.227, ...), kind=kOutput, calls=%fused_computation.16 | convolution fusion | flops 2521694208 | bytes 15751168 | tf_op jit(solution)/shard_map/dot_general | solution.py:16
  272.9 70.0 %all-gather.18.cloned.1.call-done = bf16[3072,768]{1,0:T(8,128)(2,1)} async-done(((bf16[768,768]{1,0:T(8,128)(2,1)}), bf16[3072,768]{1,0:T(8,128)(2,1)}) %all-gather.18.cloned.1.call-update) | async-done | bytes 4718608 | tf_op jit(solution)/shard_map/all_gather | solution.py:194
  342.9 6.6 fusion.39
  352.4 4.9 fusion.40
  369.0 6.8 bitcast_reduce_fusion
  378.7 6.4 multiply_reduce_fusion
  385.1 6.9 multiply_convert_fusion
  397.7 5.0 multiply_convert_fusion.1
  405.6 7.2 convolution_convert_fusion
  412.8 7.4 convolution_convert_fusion.1
  421.3 16.8 %all-reduce.18 = (bf16[768]{0:T(1024)(128)(2,1)S(1)}, bf16[768]{0:T(1024)(128)(2,1)S(1)}, bf16[768]{0:T(1024)(128)(2,1)S(1)}, bf16[768]{0:T(1024)(128)(2,1)S(1)}...) all-reduce(bf16[768]{0:T(1024)(128)(2,1)S(1)} %dynamic-update-slice, ...), channel_id=1, replica_groups=mesh['rep'=8,'fsdp'=4] {'fsdp'}, use_global_device_ids=true, to_apply=%add.7 | all-reduce | flops 9984 | bytes 39936
  451.1 19.0 %all-to-all-done.1 = bf16[32,16,768]{2,1,0:T(8,128)(2,1)S(1)} async-done(((bf16[32,16,768]{2,1,0:T(8,128)(2,1)}), bf16[32,16,768]{2,1,0:T(8,128)(2,1)S(1)}, u32[]{:S(2)}, u32[]{:S(2)}) %all-to-all-start.1) | async-done | bytes 786464 | tf_op jit(solution)/shard_map/all_to_all | solution.py:346
  470.1 5.5 all-to-all-start.3
  476.9 26.4 %all-to-all-done.3 = bf16[32,16,768]{2,1,0:T(8,128)(2,1)S(1)} async-done(((bf16[32,16,768]{2,1,0:T(8,128)(2,1)}), bf16[32,16,768]{2,1,0:T(8,128)(2,1)S(1)}, u32[]{:S(2)}, u32[]{:S(2)}) %all-to-all-start.3) | async-done | bytes 786464 | tf_op jit(solution)/shard_map/all_to_all | solution.py:347
  505.3 81.5 %reduce-scatter.17.cloned.1.call-done = bf16[768,768]{1,0:T(8,128)(2,1)} async-done(((bf16[3072,768]{1,0:T(8,128)(2,1)}), bf16[768,768]{1,0:T(8,128)(2,1)}) %reduce-scatter.17.cloned.1.call-update) | async-done | bytes 1179664 | tf_op jit(solution)/shard_map/reduce_scatter | solution.py:331
  586.8 88.0 %reduce-scatter.15.cloned.1.call-done = bf16[192,3072]{1,0:T(8,128)(2,1)} async-done(((bf16[768,3072]{1,0:T(8,128)(2,1)}), bf16[192,3072]{1,0:T(8,128)(2,1)}) %reduce-scatter.15.cloned.1.call-update) | async-done | bytes 1179664 | tf_op jit(solution)/shard_map/reduce_scatter | solution.py:325
  674.7 144.6 %all-reduce.21 = (f32[192,768]{1,0:T(8,128)}, f32[192]{0:T(256)}, f32[192,768]{1,0:T(8,128)}, f32[192,768]{1,0:T(8,128)}, f32[192]{0:T(256)}, /*index=5*/f32[192...) all-reduce(bf16[192,768]{1,0:T(8,128)(2,1)} %reduce-scatter.7.clone, ...), channel_id=1, replica_groups=mesh['rep'=8,'fsdp'=4] {'rep'}, use_global_device_ids=true, to_apply=%region_13.15 | all-reduce | flops 1771776 | bytes 10635264 | tf_op jit(solution)/shard_map/psum | solution.py:344
  (209 shorter events, 74.3 us)
Async XLA Ops:
  7.2 113.3 %all-gather.10.cloned.1.call-start = ((), (), s32[]{:S(2)}) async-start(), calls=%async_computation.11 | async-start | bytes 1474560 | tf_op jit(solution)/shard_map/all_gather | solution.py:183
  8.0 115.2 %all-gather.12.cloned.1.call-start = ((), (), s32[]{:S(2)}) async-start(), calls=%async_computation.12 | async-start | bytes 1474560 | tf_op jit(solution)/shard_map/all_gather | solution.py:185
  8.7 128.5 %all-gather.8.cloned.1.call-start = ((), (), s32[]{:S(2)}) async-start(), calls=%async_computation.10 | async-start | bytes 1474560 | tf_op jit(solution)/shard_map/all_gather | solution.py:186
  9.4 154.1 %all-gather.14.cloned.1.call-start = ((), (), s32[]{:S(2)}) async-start(), calls=%async_computation.13 | async-start | bytes 1474560 | tf_op jit(solution)/shard_map/all_gather | solution.py:188
  10.0 243.6 %all-gather.16.cloned.1.call-start = ((), (), s32[]{:S(2)}) async-start(), calls=%async_computation.14 | async-start | bytes 5898240 | tf_op jit(solution)/shard_map/all_gather | solution.py:192
  13.1 51.0 %copy-start.30 = (bf16[192]{0:T(256)(128)(2,1)S(1)}, bf16[192]{0:T(256)(128)(2,1)}, u32[]{:S(2)}) copy-start(bf16[192]{0:T(256)(128)(2,1)} %param.37) | copy-start | bytes 1156
  13.1 51.3 %copy-start.31 = (bf16[192]{0:T(256)(128)(2,1)S(1)}, bf16[192]{0:T(256)(128)(2,1)}, u32[]{:S(2)}) copy-start(bf16[192]{0:T(256)(128)(2,1)} %param.32) | copy-start | bytes 1156
  13.1 51.5 %copy-start.32 = (bf16[192]{0:T(256)(128)(2,1)S(1)}, bf16[192]{0:T(256)(128)(2,1)}, u32[]{:S(2)}) copy-start(bf16[192]{0:T(256)(128)(2,1)} %param.33) | copy-start | bytes 1156
  13.1 51.7 %copy-start.33 = (bf16[192]{0:T(256)(128)(2,1)S(1)}, bf16[192]{0:T(256)(128)(2,1)}, u32[]{:S(2)}) copy-start(bf16[192]{0:T(256)(128)(2,1)} %param.31) | copy-start | bytes 1156
  13.1 52.0 %copy-start.34 = (bf16[192]{0:T(256)(128)(2,1)S(1)}, bf16[192]{0:T(256)(128)(2,1)}, u32[]{:S(2)}) copy-start(bf16[192]{0:T(256)(128)(2,1)} %param.26) | copy-start | bytes 1156
  13.1 52.2 %copy-start.35 = (bf16[192]{0:T(256)(128)(2,1)S(1)}, bf16[192]{0:T(256)(128)(2,1)}, u32[]{:S(2)}) copy-start(bf16[192]{0:T(256)(128)(2,1)} %param.29) | copy-start | bytes 1156
  13.1 92.8 %copy-start.26 = (bf16[768]{0:T(1024)(128)(2,1)S(1)}, bf16[768]{0:T(1024)(128)(2,1)}, u32[]{:S(2)}) copy-start(bf16[768]{0:T(1024)(128)(2,1)} %param.35) | copy-start | bytes 4612
  57.5 63.0 %all-to-all-start = ((bf16[32,16,768]{2,1,0:T(8,128)(2,1)}), bf16[32,16,768]{2,1,0:T(8,128)(2,1)S(1)}, u32[]{:S(2)}, u32[]{:S(2)}) async-start(bf16[32,16,768]{2,1,0:T(8,128)(2,1)} %get-tuple-element.118), calls=%async_computation | async-start | bytes 1572864 | tf_op jit(solution)/shard_map/all_to_all | solution.py:160
  61.3 281.5 %all-gather.18.cloned.1.call-start = ((), (), s32[]{:S(2)}) async-start(), calls=%async_computation.15 | async-start | bytes 5898240 | tf_op jit(solution)/shard_map/all_gather | solution.py:194
  61.9 443.3 %reduce-scatter.13.cloned.1.call-start = ((), (), s32[]{:S(2)}) async-start(), calls=%async_computation.19 | async-start | bytes 1474560 | tf_op jit(solution)/shard_map/reduce_scatter | solution.py:313
  166.2 106.7 %copy-start.8 = (f32[512,768]{1,0:T(8,128)}, f32[512,768]{1,0:T(8,128)S(1)}, u32[]{:S(2)}) copy-start(f32[512,768]{1,0:T(8,128)S(1)} %get-tuple-element.122) | copy-start | bytes 4718596
  364.0 141.2 %reduce-scatter.11.cloned.1.call-start = ((), (), s32[]{:S(2)}) async-start(), calls=%async_computation.18 | async-start | bytes 1474560 | tf_op jit(solution)/shard_map/reduce_scatter | solution.py:307
  378.7 126.6 %reduce-scatter.7.cloned.1.call-start = ((), (), s32[]{:S(2)}) async-start(), calls=%async_computation.16 | async-start | bytes 1474560 | tf_op jit(solution)/shard_map/reduce_scatter | solution.py:298
  397.4 107.9 %reduce-scatter.9.cloned.1.call-start = ((), (), s32[]{:S(2)}) async-start(), calls=%async_computation.17 | async-start | bytes 1474560 | tf_op jit(solution)/shard_map/reduce_scatter | solution.py:304
  405.5 181.2 %reduce-scatter.17.cloned.1.call-start = ((), (), s32[]{:S(2)}) async-start(), calls=%async_computation.21 | async-start | bytes 5898240 | tf_op jit(solution)/shard_map/reduce_scatter | solution.py:331
  412.8 262.0 %reduce-scatter.15.cloned.1.call-start = ((), (), s32[]{:S(2)}) async-start(), calls=%async_computation.20 | async-start | bytes 5898240 | tf_op jit(solution)/shard_map/reduce_scatter | solution.py:325
  439.6 30.5 %all-to-all-start.1 = ((bf16[32,16,768]{2,1,0:T(8,128)(2,1)}), bf16[32,16,768]{2,1,0:T(8,128)(2,1)S(1)}, u32[]{:S(2)}, u32[]{:S(2)}) async-start(bf16[32,16,768]{2,1,0:T(8,128)(2,1)} %bitcast.10), calls=%async_computation.1 | async-start | bytes 1572864 | tf_op jit(solution)/shard_map/all_to_all | solution.py:346
  470.1 33.2 %all-to-all-start.3 = ((bf16[32,16,768]{2,1,0:T(8,128)(2,1)}), bf16[32,16,768]{2,1,0:T(8,128)(2,1)S(1)}, u32[]{:S(2)}, u32[]{:S(2)}) async-start(bf16[32,16,768]{2,1,0:T(8,128)(2,1)} %bitcast.21), calls=%async_computation.3 | async-start | bytes 1572864 | tf_op jit(solution)/shard_map/all_to_all | solution.py:347
  503.9 315.4 %copy-start.1 = (bf16[512,768]{1,0:T(8,128)(2,1)S(1)}, bf16[512,768]{1,0:T(8,128)(2,1)}, u32[]{:S(2)}) copy-start(bf16[512,768]{1,0:T(8,128)(2,1)} %param.22) | copy-start | bytes 2359300
  (34 other events, 277.9 us)
Sparse Core Ops, SparseCore 0:
  9.6 50.1 all-gather.9
  61.4 40.1 all-gather.11
  103.2 29.4 all-gather.7
  134.0 29.4 all-gather.13
  165.0 88.5 all-gather.15
  255.0 87.7 all-gather.17
  364.1 27.7 reduce-scatter.12
  394.2 27.9 reduce-scatter.10
  424.5 31.1 reduce-scatter.6
  457.9 36.0 reduce-scatter.8
  496.3 90.3 reduce-scatter.16
  588.9 85.7 reduce-scatter.14
where the time goes:
time: 831 us; the launch traced here: 827 us
  waiting for transfers between devices  390 us (47%)
  blocking collectives  260 us (31%)
  matrix products  106 us (13%)
  local copies, waits for them, and re-layouts  22.6 us (3%)
  between operations  18 us (2%)
  other arithmetic  16.4 us (2%)
  starting transfers between devices  14.3 us (2%)
    psum x1, blocking collectives, shards(): totals = lax.psum(tuple(shares), 'rep')  145 us
    reduce_scatter x1, waiting for transfers between devices, shards(): lax.psum_scatter(grad_inner_weight.astype(jnp.bfloat16), 'fsdp', scatter_...  88 us
    all_gather x1, waiting for transfers between devices, shards(): lax.all_gather(inner_weight, 'fsdp', axis=0, tiled=True)  87.1 us
    reduce_scatter x1, waiting for transfers between devices, shards(): lax.psum_scatter(grad_outer_weight.astype(jnp.bfloat16), 'fsdp', scatter_...  81.5 us
    all_gather x1, waiting for transfers between devices, shards(): lax.all_gather(outer_weight, 'fsdp', axis=0, tiled=True)  70 us
    unnamed x2, blocking collectives  57.1 us
    all_to_all x1, blocking collectives, shards(): lax.all_to_all(outgoing(cotangent), ('rep', 'fsdp'), split_axis=0, concat...  44.4 us
    dot_general x6, matrix products, matmul(): return jnp.dot(left, right, preferred_element_type=jnp.float32)  37 us
  transfers between devices with their start and end apart: 15, of which 7 were waited for; matrix products, arithmetic and copies ran while one was open for 14% of the time, Pallas kernels for 0%

commit v1 on v0

--- a/solution.py
+++ b/solution.py
@@ -1,3 +1,4 @@
+import functools
 import math
 import jax
 import jax.numpy as jnp
@@ -10,6 +11,29 @@
 masked_score = -1e30
 inv_root_two = 0.7071067811865476
 inv_root_two_pi = 0.3989422804014327
+
+
+def _derive_sectors(own_rows, along_axis, which_dim):
+    prior = lax.axis_size(along_axis)
+    arr_next = lax.axis_index(along_axis)
+    far_arr, then, current_value = (prior, arr_next, own_rows.shape[which_dim])
+    views = [(k0, (k0 + 1) % far_arr) for k0 in range(far_arr)]
+    new = jnp.zeros(
+        (*own_rows.shape[:which_dim], far_arr * current_value, *own_rows.shape[which_dim + 1 :]),
+        own_rows.dtype,
+    )
+    after = own_rows
+    rr = 0
+    while rr < far_arr:
+        taken_in = (then - rr) % far_arr
+        new = lax.dynamic_update_slice_in_dim(new, after, taken_in * current_value, axis=which_dim)
+        if rr < far_arr - 1:
+            after = lax.ppermute(after, axis_name=along_axis, perm=views)
+        rr = rr + 1
+    return new
+
+
+process_ticks_on_mesh = functools.partial(_derive_sectors, along_axis="fsdp", which_dim=0)
 
 
 def matmul(left, right):
@@ -191,7 +215,7 @@
         lax.all_gather(first_shift, "fsdp", axis=0, tiled=True),
         lax.all_gather(inner_weight, "fsdp", axis=0, tiled=True),
         lax.all_gather(inner_bias, "fsdp", axis=0, tiled=True),
-        lax.all_gather(outer_weight, "fsdp", axis=0, tiled=True),
+        process_ticks_on_mesh(outer_weight),
         lax.all_gather(outer_bias, "fsdp", axis=0, tiled=True),
         lax.all_gather(second_gain, "fsdp", axis=0, tiled=True),
         lax.all_gather(second_shift, "fsdp", axis=0, tiled=True),

time: 831 us -> 902 us (1.085)
  waiting for transfers between devices: 390 us -> 480 us
  blocking collectives: 260 us -> 217 us
  starting transfers between devices: 14.3 us -> 24.6 us
    all_to_all x0 -> x1, waiting for transfers between devices: none -> 60.2 us  [shards(): lax.all_to_all(outgoing(cotangent), ('rep', 'fsdp'), split_axis=0, concat...]
    all_to_all x1 -> x0, blocking collectives: 44.4 us -> none  [shards(): lax.all_to_all(outgoing(cotangent), ('rep', 'fsdp'), split_axis=0, concat...]
    ppermute x0 -> x3, waiting for transfers between devices: none -> 33.5 us  [_derive_sectors(): after = lax.ppermute(after, axis_name=along_axis, perm=views)]
    all_gather x1, waiting for transfers between devices: 87.1 us -> 66.1 us  [shards(): lax.all_gather(inner_weight, 'fsdp', axis=0, tiled=True)]
    dynamic_update_slice x0 -> x4, local copies, waits for them, and re-layouts: none -> 9.81 us  [_derive_sectors(): lax.dynamic_update_slice_in_dim(new, after, taken_in * current_value, axi...]
    all_gather x1, waiting for transfers between devices: 70 us -> 60.2 us  [shards(): lax.all_gather(outer_weight, 'fsdp', axis=0, tiled=True)]
  transfers between devices with their start and end apart: 15 -> 19, of which waited for: 7 -> 12; matrix products, arithmetic and copies ran while one was open for 14% -> 14% of each run, Pallas kernels for 0% -> 0%
where the time goes in v1:
time: 902 us; the launch traced here: 897 us
  waiting for transfers between devices  480 us (53%)
  blocking collectives  217 us (24%)
  matrix products  109 us (12%)
  local copies, waits for them, and re-layouts  30.5 us (3%)
  starting transfers between devices  24.6 us (3%)
  other arithmetic  18.5 us (2%)
  between operations  17.9 us (2%)
    psum x1, blocking collectives, shards(): totals = lax.psum(tuple(shares), 'rep')  145 us
    reduce_scatter x1, waiting for transfers between devices, shards(): lax.psum_scatter(grad_outer_weight.astype(jnp.bfloat16), 'fsdp', scatter_...  88 us
    reduce_scatter x1, waiting for transfers between devices, shards(): lax.psum_scatter(grad_inner_weight.astype(jnp.bfloat16), 'fsdp', scatter_...  86.8 us
    all_gather x1, waiting for transfers between devices, shards(): lax.all_gather(inner_weight, 'fsdp', axis=0, tiled=True)  66.1 us
    all_to_all x1, waiting for transfers between devices, shards(): lax.all_to_all(outgoing(cotangent), ('rep', 'fsdp'), split_axis=0, concat...  60.2 us
    all_gather x1, waiting for transfers between devices, shards(): lax.all_gather(outer_weight, 'fsdp', axis=0, tiled=True)  60.2 us
    unnamed x2, blocking collectives  58.4 us
    dot_general x6, matrix products, matmul(): return jnp.dot(left, right, preferred_element_type=jnp.float32)  37.2 us
  transfers between devices with their start and end apart: 19, of which 12 were waited for; matrix products, arithmetic and copies ran while one was open for 14% of the time, Pallas kernels for 0%

profile of v1, /device:TPU:0, one launch (start us, length us, event | category | flops | bytes accessed | tf_op | source)
XLA Modules:
  0.0 896.9 jit_solution(563433852443564842)
XLA Ops:
  14.1 7.3 all-to-all-start.2
  23.2 60.2 %all-to-all-done.2 = bf16[32,16,768]{2,1,0:T(8,128)(2,1)S(1)} async-done(((bf16[32,16,768]{2,1,0:T(8,128)(2,1)}), bf16[32,16,768]{2,1,0:T(8,128)(2,1)S(1)}, u32[]{:S(2)}, u32[]{:S(2)}) %all-to-all-start.2) | async-done | bytes 786464 | tf_op jit(solution)/shard_map/all_to_all | solution.py:185
  90.8 41.5 %all-reduce.19 = (bf16[768]{0:T(1024)(128)(2,1)S(1)}, bf16[768]{0:T(1024)(128)(2,1)S(1)}, bf16[768]{0:T(1024)(128)(2,1)S(1)}, bf16[768]{0:T(1024)(128)(2,1)S(1)}...) all-reduce(bf16[768]{0:T(1024)(128)(2,1)S(1)} %dynamic-update-slice, ...), channel_id=1, replica_groups=mesh['rep'=8,'fsdp'=4] {'fsdp'}, use_global_device_ids=true, to_apply=%add | all-reduce | flops 5376 | bytes 21504
  133.0 13.5 %all-gather = bf16[4,1,768]{2,1,0:T(2,128)(2,1)S(1)} all-gather(bf16[1,1,768]{2,1,0:T(2,128)(2,1)S(1)} %reshape.251), channel_id=1, replica_groups=mesh['rep'=8,'fsdp'=4] {'fsdp'}, dimensions={0}, use_global_device_ids=true | all-gather | bytes 7680 | tf_op jit(solution)/shard_map/all_gather | solution.py:217
  179.9 12.9 %collective-permute-done.1 = bf16[768,768]{1,0:T(8,128)(2,1)} collective-permute-done((bf16[768,768]{1,0:T(8,128)(2,1)}, bf16[768,768]{1,0:T(8,128)(2,1)}, u32[]{:S(2)}, u32[]{:S(2)}) %collective-permute-start.1) | collective-permute-done | bytes 1179680 | tf_op jit(solution)/shard_map/ppermute | solution.py:31
  195.6 14.8 %all-gather.14.cloned.1.call-done = bf16[768,768]{1,0:T(8,128)(2,1)} async-done(((bf16[192,768]{1,0:T(8,128)(2,1)}), bf16[768,768]{1,0:T(8,128)(2,1)}) %all-gather.14.cloned.1.call-update) | async-done | bytes 1179664 | tf_op jit(solution)/shard_map/all_gather | solution.py:212
  216.1 20.6 %collective-permute-done.2 = bf16[768,768]{1,0:T(8,128)(2,1)} collective-permute-done((bf16[768,768]{1,0:T(8,128)(2,1)}, bf16[768,768]{1,0:T(8,128)(2,1)}, u32[]{:S(2)}, u32[]{:S(2)}) %collective-permute-start.2) | collective-permute-done | bytes 1179680 | tf_op jit(solution)/shard_map/ppermute | solution.py:31
  239.1 66.1 %all-gather.16.cloned.1.call-done = bf16[768,3072]{1,0:T(8,128)(2,1)} async-done(((bf16[192,3072]{1,0:T(8,128)(2,1)}), bf16[768,3072]{1,0:T(8,128)(2,1)}) %all-gather.16.cloned.1.call-update) | async-done | bytes 4718608 | tf_op jit(solution)/shard_map/all_gather | solution.py:216
  305.2 19.3 %fusion.4 = (bf16[512,3072]{1,0:T(8,128)(2,1)S(1)}, f32[512,3072]{1,0:T(8,128)}) fusion(f32[3072]{0:T(1024)S(1)} %bitcast.109, bf16[768,3072]{1,0:T(8,128)(2,1)} %all-gather.16.cloned.1.call-done, f32[512,768]{1,0:T(8,128)S(1)} %get-tuple-element.122, f32[768]{0:T(1024)S(1)} %convert_element_type.228, f32[768]{0:T(1024)S(1)} %convert_element_type.227, ...), kind=kOutput, calls=%fused_computation.16 | convolution fusion | flops 2521694208 | bytes 15751168 | tf_op jit(solution)/shard_map/dot_general | solution.py:40
  324.5 6.8 fusion.39
  334.0 60.2 %all-gather.18.cloned.1.call-done = bf16[3072,768]{1,0:T(8,128)(2,1)} async-done(((bf16[768,768]{1,0:T(8,128)(2,1)}), bf16[3072,768]{1,0:T(8,128)(2,1)}) %all-gather.18.cloned.1.call-update) | async-done | bytes 4718608 | tf_op jit(solution)/shard_map/all_gather | solution.py:268
  394.2 7.9 fusion.40
  402.2 6.6 multiply_reduce_fusion.2
  413.7 6.8 bitcast_reduce_fusion
  423.3 6.9 multiply_reduce_fusion
  430.3 6.8 multiply_convert_fusion
  453.6 7.4 convolution_convert_fusion.1
  461.3 7.2 convolution_convert_fusion
  469.5 16.9 %all-reduce.18 = (bf16[768]{0:T(1024)(128)(2,1)S(1)}, bf16[768]{0:T(1024)(128)(2,1)S(1)}, bf16[768]{0:T(1024)(128)(2,1)S(1)}, bf16[768]{0:T(1024)(128)(2,1)S(1)}...) all-reduce(bf16[768]{0:T(1024)(128)(2,1)S(1)} %dynamic-update-slice, ...), channel_id=1, replica_groups=mesh['rep'=8,'fsdp'=4] {'fsdp'}, use_global_device_ids=true, to_apply=%add.7 | all-reduce | flops 9984 | bytes 39936
  499.4 27.8 %all-to-all-done.1 = bf16[32,16,768]{2,1,0:T(8,128)(2,1)S(1)} async-done(((bf16[32,16,768]{2,1,0:T(8,128)(2,1)}), bf16[32,16,768]{2,1,0:T(8,128)(2,1)S(1)}, u32[]{:S(2)}, u32[]{:S(2)}) %all-to-all-start.1) | async-done | bytes 786464 | tf_op jit(solution)/shard_map/all_to_all | solution.py:370
  532.3 31.8 %all-to-all-done.3 = bf16[32,16,768]{2,1,0:T(8,128)(2,1)S(1)} async-done(((bf16[32,16,768]{2,1,0:T(8,128)(2,1)}), bf16[32,16,768]{2,1,0:T(8,128)(2,1)S(1)}, u32[]{:S(2)}, u32[]{:S(2)}) %all-to-all-start.3) | async-done | bytes 786464 | tf_op jit(solution)/shard_map/all_to_all | solution.py:371
  570.5 86.8 %reduce-scatter.15.cloned.1.call-done = bf16[192,3072]{1,0:T(8,128)(2,1)} async-done(((bf16[768,3072]{1,0:T(8,128)(2,1)}), bf16[192,3072]{1,0:T(8,128)(2,1)}) %reduce-scatter.15.cloned.1.call-update) | async-done | bytes 1179664 | tf_op jit(solution)/shard_map/reduce_scatter | solution.py:349
  657.3 88.0 %reduce-scatter.17.cloned.1.call-done = bf16[768,768]{1,0:T(8,128)(2,1)} async-done(((bf16[3072,768]{1,0:T(8,128)(2,1)}), bf16[768,768]{1,0:T(8,128)(2,1)}) %reduce-scatter.17.cloned.1.call-update) | async-done | bytes 1179664 | tf_op jit(solution)/shard_map/reduce_scatter | solution.py:355
  745.3 144.6 %all-reduce.21 = (f32[192,768]{1,0:T(8,128)}, f32[192]{0:T(256)}, f32[192,768]{1,0:T(8,128)}, f32[192,768]{1,0:T(8,128)}, f32[192]{0:T(256)}, /*index=5*/f32[192...) all-reduce(bf16[192,768]{1,0:T(8,128)(2,1)} %reduce-scatter.7.clone, ...), channel_id=1, replica_groups=mesh['rep'=8,'fsdp'=4] {'rep'}, use_global_device_ids=true, to_apply=%region_13.15 | all-reduce | flops 1771776 | bytes 10635264 | tf_op jit(solution)/shard_map/psum | solution.py:368
  (212 shorter events, 110.3 us)
Async XLA Ops:
  7.2 147.7 %all-gather.10.cloned.1.call-start = ((), (), s32[]{:S(2)}) async-start(), calls=%async_computation.11 | async-start | bytes 1474560 | tf_op jit(solution)/shard_map/all_gather | solution.py:207
  8.0 149.6 %all-gather.12.cloned.1.call-start = ((), (), s32[]{:S(2)}) async-start(), calls=%async_computation.12 | async-start | bytes 1474560 | tf_op jit(solution)/shard_map/all_gather | solution.py:209
  8.7 156.1 %all-gather.8.cloned.1.call-start = ((), (), s32[]{:S(2)}) async-start(), calls=%async_computation.10 | async-start | bytes 1474560 | tf_op jit(solution)/shard_map/all_gather | solution.py:210
  9.4 201.0 %all-gather.14.cloned.1.call-start = ((), (), s32[]{:S(2)}) async-start(), calls=%async_computation.13 | async-start | bytes 1474560 | tf_op jit(solution)/shard_map/all_gather | solution.py:212
  10.0 295.2 %all-gather.16.cloned.1.call-start = ((), (), s32[]{:S(2)}) async-start(), calls=%async_computation.14 | async-start | bytes 5898240 | tf_op jit(solution)/shard_map/all_gather | solution.py:216
  12.7 77.6 %copy-start.33 = (bf16[192]{0:T(256)(128)(2,1)S(1)}, bf16[192]{0:T(256)(128)(2,1)}, u32[]{:S(2)}) copy-start(bf16[192]{0:T(256)(128)(2,1)} %param.37) | copy-start | bytes 1156
  12.7 77.8 %copy-start.34 = (bf16[192]{0:T(256)(128)(2,1)S(1)}, bf16[192]{0:T(256)(128)(2,1)}, u32[]{:S(2)}) copy-start(bf16[192]{0:T(256)(128)(2,1)} %param.38) | copy-start | bytes 1156
  12.7 120.2 %copy-start.26 = (bf16[768]{0:T(1024)(128)(2,1)S(1)}, bf16[768]{0:T(1024)(128)(2,1)}, u32[]{:S(2)}) copy-start(bf16[768]{0:T(1024)(128)(2,1)} %param.35) | copy-start | bytes 4612
  14.1 69.3 %all-to-all-start.2 = ((bf16[32,16,768]{2,1,0:T(8,128)(2,1)}), bf16[32,16,768]{2,1,0:T(8,128)(2,1)S(1)}, u32[]{:S(2)}, u32[]{:S(2)}) async-start(bf16[32,16,768]{2,1,0:T(8,128)(2,1)} %get-tuple-element.117), calls=%async_computation.2 | async-start | bytes 1572864 | tf_op jit(solution)/shard_map/all_to_all | solution.py:185
  21.4 130.0 %collective-permute-start = (bf16[768,768]{1,0:T(8,128)(2,1)}, bf16[768,768]{1,0:T(8,128)(2,1)}, u32[]{:S(2)}, u32[]{:S(2)}) collective-permute-start(bf16[768,768]{1,0:T(8,128)(2,1)} %param.36), channel_id=1, source_target_pairs={{0,1},{1,2},{2,3},{3,0},{4,5},{5,6},{6,7},{7,4},{8,9},{9,10},{10,1... | collective-permute-start | bytes 3538952 | tf_op jit(solution)/shard_map/ppermute | solution.py:31
  83.4 71.4 %all-to-all-start = ((bf16[32,16,768]{2,1,0:T(8,128)(2,1)}), bf16[32,16,768]{2,1,0:T(8,128)(2,1)S(1)}, u32[]{:S(2)}, u32[]{:S(2)}) async-start(bf16[32,16,768]{2,1,0:T(8,128)(2,1)} %get-tuple-element.118), calls=%async_computation | async-start | bytes 1572864 | tf_op jit(solution)/shard_map/all_to_all | solution.py:184
  87.1 307.1 %all-gather.18.cloned.1.call-start = ((), (), s32[]{:S(2)}) async-start(), calls=%async_computation.15 | async-start | bytes 5898240 | tf_op jit(solution)/shard_map/all_gather | solution.py:268
  87.7 478.3 %reduce-scatter.11.cloned.1.call-start = ((), (), s32[]{:S(2)}) async-start(), calls=%async_computation.18 | async-start | bytes 1474560 | tf_op jit(solution)/shard_map/reduce_scatter | solution.py:331
  151.4 41.4 %collective-permute-start.1 = (bf16[768,768]{1,0:T(8,128)(2,1)}, bf16[768,768]{1,0:T(8,128)(2,1)}, u32[]{:S(2)}, u32[]{:S(2)}) collective-permute-start(bf16[768,768]{1,0:T(8,128)(2,1)} %collective-permute-done), channel_id=1, source_target_pairs={{0,1},{1,2},{2,3},{3,0},{4,5},{5,6},{6,7},{7,4},{8,9},{9,10},{10,1... | collective-permute-start | bytes 3538952 | tf_op jit(solution)/shard_map/ppermute | solution.py:31
  192.8 43.9 %collective-permute-start.2 = (bf16[768,768]{1,0:T(8,128)(2,1)}, bf16[768,768]{1,0:T(8,128)(2,1)}, u32[]{:S(2)}, u32[]{:S(2)}) collective-permute-start(bf16[768,768]{1,0:T(8,128)(2,1)} %collective-permute-done.1), channel_id=1, source_target_pairs={{0,1},{1,2},{2,3},{3,0},{4,5},{5,6},{6,7},{7,4},{8,9},{9,10},{10,1... | collective-permute-start | bytes 3538952 | tf_op jit(solution)/shard_map/ppermute | solution.py:31
  213.1 92.1 %copy-start.8 = (f32[512,768]{1,0:T(8,128)}, f32[512,768]{1,0:T(8,128)S(1)}, u32[]{:S(2)}) copy-start(f32[512,768]{1,0:T(8,128)S(1)} %get-tuple-element.122) | copy-start | bytes 4718596
  423.3 142.8 %reduce-scatter.7.cloned.1.call-start = ((), (), s32[]{:S(2)}) async-start(), calls=%async_computation.16 | async-start | bytes 1474560 | tf_op jit(solution)/shard_map/reduce_scatter | solution.py:322
  442.6 123.5 %reduce-scatter.9.cloned.1.call-start = ((), (), s32[]{:S(2)}) async-start(), calls=%async_computation.17 | async-start | bytes 1474560 | tf_op jit(solution)/shard_map/reduce_scatter | solution.py:328
  450.3 120.3 %reduce-scatter.13.cloned.1.call-start = ((), (), s32[]{:S(2)}) async-start(), calls=%async_computation.19 | async-start | bytes 1474560 | tf_op jit(solution)/shard_map/reduce_scatter | solution.py:337
  453.6 203.7 %reduce-scatter.15.cloned.1.call-start = ((), (), s32[]{:S(2)}) async-start(), calls=%async_computation.20 | async-start | bytes 5898240 | tf_op jit(solution)/shard_map/reduce_scatter | solution.py:349
  461.0 284.2 %reduce-scatter.17.cloned.1.call-start = ((), (), s32[]{:S(2)}) async-start(), calls=%async_computation.21 | async-start | bytes 5898240 | tf_op jit(solution)/shard_map/reduce_scatter | solution.py:355
  488.0 39.2 %all-to-all-start.1 = ((bf16[32,16,768]{2,1,0:T(8,128)(2,1)}), bf16[32,16,768]{2,1,0:T(8,128)(2,1)S(1)}, u32[]{:S(2)}, u32[]{:S(2)}) async-start(bf16[32,16,768]{2,1,0:T(8,128)(2,1)} %bitcast.10), calls=%async_computation.1 | async-start | bytes 1572864 | tf_op jit(solution)/shard_map/all_to_all | solution.py:370
  527.2 36.9 %all-to-all-start.3 = ((bf16[32,16,768]{2,1,0:T(8,128)(2,1)}), bf16[32,16,768]{2,1,0:T(8,128)(2,1)S(1)}, u32[]{:S(2)}, u32[]{:S(2)}) async-start(bf16[32,16,768]{2,1,0:T(8,128)(2,1)} %bitcast.21), calls=%async_computation.3 | async-start | bytes 1572864 | tf_op jit(solution)/shard_map/all_to_all | solution.py:371
  564.1 325.8 %copy-start.1 = (bf16[512,768]{1,0:T(8,128)(2,1)S(1)}, bf16[512,768]{1,0:T(8,128)(2,1)}, u32[]{:S(2)}) copy-start(bf16[512,768]{1,0:T(8,128)(2,1)} %param.21) | copy-start | bytes 2359300
  (34 other events, 639.5 us)
Sparse Core Ops, SparseCore 0:
  9.6 75.4 all-gather.9
  86.6 40.6 all-gather.11
  128.9 35.7 all-gather.7
  166.2 44.2 all-gather.13
  211.9 93.2 all-gather.15
  306.6 87.5 all-gather.17
  423.4 27.7 reduce-scatter.10
  453.5 28.6 reduce-scatter.6
  484.5 40.5 reduce-scatter.8
  527.2 43.2 reduce-scatter.12
  572.8 84.4 reduce-scatter.14
  659.5 85.7 reduce-scatter.16
